TPU v7x, 32 devices: a whole 2x2x4 slice. The times are simulated.
32 devices in a mesh: groups: 2 (over x), cent: 16 (over z, y, core).
Axes of the slice: x: 2, y: 2, z: 4, core: 2. Of those that a mesh axis runs over, the one named last changes fastest.
Arguments:
- points: bfloat16 [1024, 768], P(('groups', 'cent')), parts along dimension 0, may hold values from -64 to 64, as said below
- centroids: bfloat16 [131072, 768], P(('groups', 'cent')), parts along dimension 0, may hold values from -1 to 1
- coarse_init: float32 [4096, 768], P(('groups', 'cent')), parts along dimension 0, may hold values from -2.4 to 2.4
- assign: int32 [131072], P(('groups', 'cent')), parts along dimension 0, may hold values from 0 to 2047, as said below
Outputs:
- level_one: bfloat16 [131072, 768], P(('groups', 'cent')), parts along dimension 0
- level_two: float32 [4096, 768], P(('groups', 'cent')), parts along dimension 0
There are 2 independent parts, one for each index of `groups`. A program takes and returns all parts, laid end to end along the dimension named above; each array names one. Nothing has to cross between parts.
Inputs may be any that keep to these rules, and one draw needn't show every extreme that they name: `points`: entries normal (clipped at 8) or uniform within 1.7; on some draws a few rows are scaled multiples of a centroid that has a close twin, giving logits up to about 300. `assign`: among the 65536 // 16 level-1 centroids held by one index of cent, at most 512 have their level-2 centroid in any one block of 2048 // 16 consecutive level-2 centroids, and some block receives exactly 512.
All inputs are finite; a program needn't handle non-finite values.
Results may differ from a plain program's by a relative error of at most 0.0039.
Values may be sent and summed in bfloat16 or wider, within the bound.
A program may use at most 64 MiB of HBM per device.

v0:
```python
import functools
import math

import jax
import jax.numpy as jnp
from jax import lax
from jax.experimental import pallas as pl
from jax.experimental.pallas import tpu as pltpu
from jax.sharding import PartitionSpec as P

TEMP = 0.05
PRIOR_ONE = 0.02
PRIOR_TWO = 0.25
LANES = 128
MESH = pl.DeviceIdType.MESH
ROWS_BY_ROWS = (((1,), (1,)), ((), ()))


def log2_scale(width):
    return math.log2(math.e) / (TEMP * math.sqrt(width))


def stats_kernel(n, tile, pts_ref, cen_hbm, all_ref, lse_ref, cen, mine, theirs, cen_sem, sems):
    group, me = lax.axis_index("groups"), lax.axis_index("cent")
    rows, width = pts_ref.shape
    count = all_ref.shape[0]
    tiles = cen.shape[0] // tile
    c2 = log2_scale(width)

    def fetch(t):
        part = pl.ds(t * tile, tile)
        return pltpu.make_async_copy(cen_hbm.at[part], cen.at[part], cen_sem.at[t])

    for t in range(tiles):
        fetch(t).start()

    barrier = pltpu.get_barrier_semaphore()

    @pl.loop(1, n)
    def _(off):
        peer = lax.rem(me + off, n)
        pl.semaphore_signal(barrier, inc=1, device_id=(group, peer), device_id_type=MESH)

    pl.semaphore_wait(barrier, n - 1)

    here = pl.ds(pl.multiple_of(me * rows, rows), rows)

    @pl.loop(1, n)
    def _(off):
        pltpu.make_async_remote_copy(
            src_ref=pts_ref,
            dst_ref=all_ref.at[here],
            send_sem=sems.at[0],
            recv_sem=sems.at[1],
            device_id=(group, lax.rem(me + off, n)),
            device_id_type=MESH,
        ).start()

    all_ref[here, :] = pts_ref[...]
    others = all_ref.at[pl.ds(0, (n - 1) * rows)]
    pltpu.make_async_copy(others, others, sems.at[1]).wait()

    peak = jnp.full((1, count), -jnp.inf, jnp.float32)
    total = jnp.zeros((1, count), jnp.float32)

    def step(t, carry):
        peak, total = carry
        fetch(t).wait()
        block = cen[pl.ds(pl.multiple_of(t * tile, tile), tile), :]
        logits = (
            lax.dot_general(block, all_ref[...], ROWS_BY_ROWS, preferred_element_type=jnp.float32)
            * c2
        )
        higher = jnp.maximum(peak, jnp.max(logits, axis=0, keepdims=True))
        total = total * jnp.exp2(peak - higher) + jnp.sum(
            jnp.exp2(logits - higher), axis=0, keepdims=True
        )
        return higher, total

    peak, total = lax.fori_loop(0, tiles, step, (peak, total))
    mine[0:1, :] = peak
    mine[1:2, :] = total

    @pl.loop(1, n)
    def _(off):
        pltpu.make_async_remote_copy(
            src_ref=mine,
            dst_ref=theirs.at[off - 1],
            send_sem=sems.at[2],
            recv_sem=sems.at[3],
            device_id=(group, lax.rem(me + off, n)),
            device_id_type=MESH,
        ).start()

    pltpu.make_async_copy(theirs, theirs, sems.at[3]).wait()
    both = theirs[...]
    top = jnp.maximum(peak, jnp.max(both[:, 0:1, :], axis=0))
    denom = total * jnp.exp2(peak - top) + jnp.sum(
        both[:, 1:2, :] * jnp.exp2(both[:, 0:1, :] - top[None]), axis=0
    )
    lse_ref[...] = top + jnp.log2(denom)
    pltpu.make_async_copy(others, others, sems.at[0]).wait()
    pltpu.make_async_copy(theirs, theirs, sems.at[2]).wait()


def update_kernel(cen_ref, pts_ref, lse_ref, one_ref, moved_ref, mass_ref):
    tile, width = cen_ref.shape
    cen, pts = cen_ref[...], pts_ref[...]
    logits = lax.dot_general(cen, pts, ROWS_BY_ROWS, preferred_element_type=jnp.float32)
    resp = jnp.exp2(logits * log2_scale(width) - lse_ref[...])
    mass = jnp.sum(resp, axis=1, keepdims=True)
    weighted = jnp.dot(resp.astype(jnp.bfloat16), pts, preferred_element_type=jnp.float32)
    fresh = (weighted + PRIOR_ONE * cen.astype(jnp.float32)) * (1.0 / (mass + PRIOR_ONE))
    one_ref[...] = fresh.astype(jnp.bfloat16)
    moved_ref[...] = (mass * fresh).astype(jnp.bfloat16)
    mass_ref[...] = jnp.broadcast_to(mass, (tile, LANES)).T[0:1, :]


def coarse_kernel(
    n,
    moved_hbm,
    mass_ref,
    assign_ref,
    init_ref,
    two_ref,
    moved,
    core_out,
    core_in,
    line_out,
    line_in,
    total,
    pair_out,
    pair_in,
    moved_sem,
    core_sem,
    line_sem,
    pair_sem,
):
    group, me = lax.axis_index("groups"), lax.axis_index("cent")
    own, width = init_ref.shape
    lines = n // 4
    line, pair, core = me // 4, lax.rem(me // 2, 2), lax.rem(me, 2)

    def at(z, y, c):
        return (group, z * 4 + y * 2 + c)

    load = pltpu.make_async_copy(moved_hbm, moved, moved_sem)
    load.start()
    barrier = pltpu.get_barrier_semaphore()

    def greet(who):
        pl.semaphore_signal(barrier, inc=1, device_id=who, device_id_type=MESH)

    greet(at(line, pair, 1 - core))
    greet(at(line, 1 - pair, core))

    @pl.loop(1, lines)
    def _(off):
        greet(at(lax.rem(line + off, lines), pair, core))

    pl.semaphore_wait(barrier, lines + 1)
    load.wait()

    lane = lax.broadcasted_iota(jnp.int32, (2 * own, LANES), 1)

    def partial(z, c):
        base = z * (4 * own) + c * own
        row = lax.broadcasted_iota(jnp.int32, (2 * own, 1), 0)
        row = jnp.where(row >= own, row + own, row)
        hit = (assign_ref[...] - base) == row
        weight = jnp.sum(jnp.where(hit, mass_ref[...], 0.0), axis=1, keepdims=True)
        onehot = jnp.where(hit, 1.0, 0.0).astype(jnp.bfloat16)
        return jnp.dot(onehot, moved[...], preferred_element_type=jnp.float32), weight

    def put(dst, sums, weight):
        high = weight.astype(jnp.bfloat16).astype(jnp.float32)
        low = weight - high
        at_lane = lane[: weight.shape[0]]
        tail = jnp.where(at_lane == 0, high, jnp.where(at_lane == 1, low, 0.0))
        dst[:, :width] = sums.astype(jnp.bfloat16)
        dst[:, width:] = tail.astype(jnp.bfloat16)

    def get(src):
        tail = src[:, width:].astype(jnp.float32)
        return src[:, :width].astype(jnp.float32), jnp.sum(tail, axis=1, keepdims=True)

    def core_copy(s):
        return pltpu.make_async_remote_copy(
            src_ref=core_out.at[s],
            dst_ref=core_in.at[s],
            send_sem=core_sem.at[0, s],
            recv_sem=core_sem.at[1, s],
            device_id=at(line, pair, 1 - core),
            device_id_type=MESH,
        )

    def line_copy(s):
        return pltpu.make_async_remote_copy(
            src_ref=line_out.at[s],
            dst_ref=line_in.at[s],
            send_sem=line_sem.at[0, s],
            recv_sem=line_sem.at[1, s],
            device_id=at(lax.rem(line + 1 + s, lines), pair, core),
            device_id_type=MESH,
        )

    @pl.loop(0, lines)
    def _(s):
        z = lax.rem(line + 1 + s, lines)
        put(core_out.at[s], *partial(z, 1 - core))
        core_copy(s).start()
        sums, weight = partial(z, core)
        total[:, :width] = sums
        core_copy(s).wait_recv()
        other, other_weight = get(core_in.at[s])
        sums = total[:, :width] + other
        weight = weight + other_weight

        @pl.when(s < lines - 1)
        def _():
            put(line_out.at[s], sums, weight)
            line_copy(s).start()

        @pl.when(s == lines - 1)
        def _():
            total[:, :width] = sums
            total[:, width:] = jnp.broadcast_to(weight, (2 * own, LANES))

    @pl.loop(0, lines - 1)
    def _(s):
        line_copy(s).wait_recv()
        sums, weight = get(line_in.at[s])
        total[:, :width] = total[:, :width] + sums
        total[:, width:] = total[:, width:] + weight

    def half(y):
        rows = pl.ds(pl.multiple_of(y * own, own), own)
        return total[rows, :width], total[rows, width : width + 1]

    put(pair_out, *half(1 - pair))
    swap = pltpu.make_async_remote_copy(
        src_ref=pair_out,
        dst_ref=pair_in,
        send_sem=pair_sem.at[0],
        recv_sem=pair_sem.at[1],
        device_id=at(line, 1 - pair, core),
        device_id_type=MESH,
    )
    swap.start()
    swap.wait_recv()
    sums, weight = half(pair)
    other, other_weight = get(pair_in)
    weight = weight + other_weight
    two_ref[...] = (sums + other + PRIOR_TWO * init_ref[...]) / (weight + PRIOR_TWO)

    @pl.loop(0, lines)
    def _(s):
        core_copy(s).wait_send()

    @pl.loop(0, lines - 1)
    def _(s):
        line_copy(s).wait_send()

    swap.wait_send()


def shards(n, points, centroids, coarse_init, assign):
    rows, width = points.shape
    local = centroids.shape[0]
    own = coarse_init.shape[0]
    count = n * rows
    tile = min(512, local)
    vmem = pl.BlockSpec(memory_space=pltpu.VMEM)
    anywhere = pl.BlockSpec(memory_space=pl.ANY)
    everyone, lse = pl.pallas_call(
        functools.partial(stats_kernel, n, tile),
        out_shape=(
            jax.ShapeDtypeStruct((count, width), jnp.bfloat16),
            jax.ShapeDtypeStruct((1, count), jnp.float32),
        ),
        in_specs=[vmem, anywhere],
        out_specs=(vmem, vmem),
        scratch_shapes=[
            pltpu.VMEM((local, width), jnp.bfloat16),
            pltpu.VMEM((2, count), jnp.float32),
            pltpu.VMEM((n - 1, 2, count), jnp.float32),
            pltpu.SemaphoreType.DMA((local // tile,)),
            pltpu.SemaphoreType.DMA((4,)),
        ],
        compiler_params=pltpu.CompilerParams(collective_id=0, has_side_effects=True),
        name="stats",
    )(points, centroids)
    level_one, moved, mass = pl.pallas_call(
        update_kernel,
        grid=(local // tile,),
        out_shape=(
            jax.ShapeDtypeStruct((local, width), jnp.bfloat16),
            jax.ShapeDtypeStruct((local, width), jnp.bfloat16),
            jax.ShapeDtypeStruct((1, local), jnp.float32),
        ),
        in_specs=[
            pl.BlockSpec((tile, width), lambda t: (t, 0)),
            pl.BlockSpec((count, width), lambda t: (0, 0)),
            pl.BlockSpec((1, count), lambda t: (0, 0)),
        ],
        out_specs=(
            pl.BlockSpec((tile, width), lambda t: (t, 0)),
            pl.BlockSpec((tile, width), lambda t: (t, 0)),
            pl.BlockSpec((1, tile), lambda t: (0, t)),
        ),
        name="update",
    )(centroids, everyone, lse)
    lines = n // 4
    wide = width + LANES
    level_two = pl.pallas_call(
        functools.partial(coarse_kernel, n),
        out_shape=jax.ShapeDtypeStruct((own, width), jnp.float32),
        in_specs=[anywhere, vmem, vmem, vmem],
        out_specs=vmem,
        scratch_shapes=[
            pltpu.VMEM((local, width), jnp.bfloat16),
            pltpu.VMEM((lines, 2 * own, wide), jnp.bfloat16),
            pltpu.VMEM((lines, 2 * own, wide), jnp.bfloat16),
            pltpu.VMEM((lines, 2 * own, wide), jnp.bfloat16),
            pltpu.VMEM((lines, 2 * own, wide), jnp.bfloat16),
            pltpu.VMEM((2 * own, wide), jnp.float32),
            pltpu.VMEM((own, wide), jnp.bfloat16),
            pltpu.VMEM((own, wide), jnp.bfloat16),
            pltpu.SemaphoreType.DMA,
            pltpu.SemaphoreType.DMA((2, lines)),
            pltpu.SemaphoreType.DMA((2, lines)),
            pltpu.SemaphoreType.DMA((2,)),
        ],
        compiler_params=pltpu.CompilerParams(collective_id=1, has_side_effects=True),
        name="coarse",
    )(moved, mass, assign.reshape(1, local), coarse_init)
    return (level_one, level_two)


def solution(mesh):
    return jax.shard_map(
        functools.partial(shards, mesh.shape["cent"]),
        mesh=mesh,
        in_specs=(
            P(("groups", "cent"), None),
            P(("groups", "cent"), None),
            P(("groups", "cent"), None),
            P(("groups", "cent")),
        ),
        out_specs=(P(("groups", "cent"), None), P(("groups", "cent"), None)),
        check_vma=False,
    )
```

profile of v0, /device:TPU:10, one launch (start us, length us, event | category | flops | bytes accessed | tf_op | source)
XLA Modules:
  0.0 108.7 jit_solution(11141153494256438545)
XLA Ops:
  0.6 35.0 %stats.1 = (bf16[512,768]{1,0:T(8,128)(2,1)}, f32[1,512]{1,0:T(1,128)}) custom-call(bf16[32,768]{1,0:T(8,128)(2,1)} %pts_ref.1, bf16[4096,768]{1,0:T(8,128)(2,1)} %cen_ref.1), custom_call_target="tpu_custom_call" | custom-call | tf_op jit(solution)/shard_map/stats/pallas_call | solution.py:275
  35.6 13.8 %update.1 = (bf16[4096,768]{1,0:T(8,128)(2,1)}, bf16[4096,768]{1,0:T(8,128)(2,1)}, f32[1,4096]{1,0:T(1,128)}) custom-call(bf16[4096,768]{1,0:T(8,128)(2,1)} %cen_ref.1, bf16[512,768]{1,0:T(8,128)(2,1)} %get-tuple-element.7.pts_ref, f32[1,512]{1,0:T(1,128)} %get-tuple-element.8.lse_ref), custom_call_target="tpu_custom_call" | custom-call | tf_op jit(solution)/shard_map/update/pallas_call | solution.py:293
  49.4 57.6 %coarse.1 = f32[128,768]{1,0:T(8,128)} custom-call(bf16[4096,768]{1,0:T(8,128)(2,1)} %get-tuple-element.10.moved_hbm, f32[1,4096]{1,0:T(1,128)} %get-tuple-element.11.mass_ref, s32[1,4096]{1,0:T(1,128)} %bitcast.1, f32[128,768]{1,0:T(8,128)} %init_ref.1), custom_call_target="tpu_custom_call" | custom-call | tf_op jit(solution)/shard_map/coarse/pallas_call | solution.py:315
  107.0 1.8 %copy.7 = f32[128,768]{1,0:T(8,128)} copy(f32[128,768]{1,0:T(8,128)} %coarse.1) | data formatting | bytes 786432
where the time goes:
time: 109 us
  Pallas kernels  106 us (97%)
  local copies, waits for them, and re-layouts  1.77 us (2%)
    pallas_call x1, Pallas kernels, shards(): pl.pallas_call(functools.partial(coarse_kernel, n), out_shape=jax.ShapeDt...  57.6 us
    pallas_call x1, Pallas kernels, shards(): pl.pallas_call(functools.partial(stats_kernel, n, tile), out_shape=(jax.S...  35 us
    pallas_call x1, Pallas kernels, shards(): pl.pallas_call(update_kernel, grid=(local // tile,), out_shape=(jax.Shape...  13.8 us

commit v1 on v0

v1 whole, which is shorter than its diff:
```python
import functools
import math

import jax
import jax.numpy as jnp
from jax import lax
from jax.experimental import pallas as pl
from jax.experimental.pallas import tpu as pltpu
from jax.sharding import PartitionSpec as P

TEMP = 0.05
PRIOR_ONE = 0.02
PRIOR_TWO = 0.25
LANES = 128
MESH = pl.DeviceIdType.MESH
ROWS_BY_ROWS = (((1,), (1,)), ((), ()))


def log2_scale(width):
    return math.log2(math.e) / (TEMP * math.sqrt(width))


def flip(z, e, lines):
    out, bit = 0, 1
    while bit < lines:
        out = out + bit * lax.rem(z // bit + e // bit, 2)
        bit *= 2
    return out


def stats_kernel(
    n, tile, pts_ref, cen_hbm, all_ref, lse_ref, cen, mine, theirs, cen_sem, line_sem, pair_sem, core_sem, sems
):
    group, me = lax.axis_index("groups"), lax.axis_index("cent")
    rows, width = pts_ref.shape
    part = rows // 2
    count = n * part
    lines = n // 4
    line, pair, core = me // 4, lax.rem(me // 2, 2), lax.rem(me, 2)
    tiles = cen.shape[0] // tile
    c2 = log2_scale(width)

    def fetch(t):
        part_of = pl.ds(t * tile, tile)
        return pltpu.make_async_copy(cen_hbm.at[part_of], cen.at[part_of], cen_sem.at[t])

    for t in range(tiles):
        fetch(t).start()

    barrier = pltpu.get_barrier_semaphore()

    @pl.loop(1, n)
    def _(off):
        peer = lax.rem(me + off, n)
        pl.semaphore_signal(barrier, inc=1, device_id=(group, peer), device_id_type=MESH)

    pl.semaphore_wait(barrier, n - 1)

    def slot(h, z, y, c):
        return pl.ds(pl.multiple_of(h * count + (z * 4 + y * 2 + c) * part, part), part)

    def send(src, where, sem, z, y, c):
        return pltpu.make_async_remote_copy(
            src_ref=src,
            dst_ref=all_ref.at[where],
            send_sem=sems.at[0],
            recv_sem=sem,
            device_id=(group, z * 4 + y * 2 + c),
            device_id_type=MESH,
        )

    def along(h, e, src, where):
        z = flip(line, e, lines)
        return send(src, where, line_sem.at[h, e], z, pair, core)

    def across(h, e, src, where):
        return send(src, where, pair_sem.at[h, e], line, 1 - pair, core)

    def over(h, src, where):
        return send(src, where, core_sem.at[h], line, pair, 1 - core)

    def relay_line(h):
        for e in range(1, lines):
            where = slot(h, flip(line, e, lines), pair, core)
            got = all_ref.at[where]
            along(h, e, got, where).wait_recv()
            across(h, e, got, where).start()
            over(h, got, where).start()

    def relay_pair(h):
        for e in range(lines):
            where = slot(h, flip(line, e, lines), 1 - pair, core)
            got = all_ref.at[where]
            across(h, e, got, where).wait_recv()
            over(h, got, where).start()

    def gathered(h):
        whole = all_ref.at[pl.ds(0, 2 * lines * part)]
        pltpu.make_async_copy(whole, whole, core_sem.at[h]).wait()

    for h in range(2):
        own = pts_ref.at[pl.ds(h * part, part)]
        where = slot(h, line, pair, core)
        for e in range(lines - 1, 0, -1):
            along(h, e, own, where).start()
        across(h, 0, own, where).start()
        over(h, own, where).start()
        all_ref[where, :] = pts_ref[pl.ds(h * part, part), :]

    def stats(h, first, last, carry):
        def step(t, carry):
            peak, total = carry
            if h == 0:
                fetch(t).wait()
            block = cen[pl.ds(pl.multiple_of(t * tile, tile), tile), :]
            pts = all_ref[pl.ds(h * count, count), :]
            logits = (
                lax.dot_general(block, pts, ROWS_BY_ROWS, preferred_element_type=jnp.float32) * c2
            )
            higher = jnp.maximum(peak, jnp.max(logits, axis=0, keepdims=True))
            total = total * jnp.exp2(peak - higher) + jnp.sum(
                jnp.exp2(logits - higher), axis=0, keepdims=True
            )
            return higher, total

        return lax.fori_loop(first, last, step, carry)

    def share(h, off):
        return pltpu.make_async_remote_copy(
            src_ref=mine.at[h],
            dst_ref=theirs.at[h, off - 1],
            send_sem=sems.at[1],
            recv_sem=sems.at[2 + h],
            device_id=(group, lax.rem(me + off, n)),
            device_id_type=MESH,
        )

    def publish(h, carry):
        peak, total = carry
        mine[h, 0:1, :] = peak
        mine[h, 1:2, :] = total

        @pl.loop(1, n)
        def _(off):
            share(h, off).start()

    def merge(h, carry):
        peak, total = carry
        got = theirs.at[h]
        pltpu.make_async_copy(got, got, sems.at[2 + h]).wait()
        both = theirs[h]
        top = jnp.maximum(peak, jnp.max(both[:, 0:1, :], axis=0))
        denom = total * jnp.exp2(peak - top) + jnp.sum(
            both[:, 1:2, :] * jnp.exp2(both[:, 0:1, :] - top[None]), axis=0
        )
        lse_ref[:, pl.ds(h * count, count)] = top + jnp.log2(denom)

    start = (jnp.full((1, count), -jnp.inf, jnp.float32), jnp.zeros((1, count), jnp.float32))
    relay_line(0)
    relay_line(1)
    relay_pair(0)
    gathered(0)
    carry0 = stats(0, 0, tiles // 2, start)
    relay_pair(1)
    carry0 = stats(0, tiles // 2, tiles, carry0)
    publish(0, carry0)
    gathered(1)
    carry1 = stats(1, 0, tiles, start)
    publish(1, carry1)
    merge(0, carry0)
    merge(1, carry1)
    others = all_ref.at[pl.ds(0, (n - 1) * rows)]
    pltpu.make_async_copy(others, others, sems.at[0]).wait()
    pltpu.make_async_copy(theirs, theirs, sems.at[1]).wait()


def update_kernel(cen_ref, pts_ref, lse_ref, one_ref, moved_ref, mass_ref):
    tile, width = cen_ref.shape
    cen, pts = cen_ref[...], pts_ref[...]
    logits = lax.dot_general(cen, pts, ROWS_BY_ROWS, preferred_element_type=jnp.float32)
    resp = jnp.exp2(logits * log2_scale(width) - lse_ref[...])
    mass = jnp.sum(resp, axis=1, keepdims=True)
    weighted = jnp.dot(resp.astype(jnp.bfloat16), pts, preferred_element_type=jnp.float32)
    fresh = (weighted + PRIOR_ONE * cen.astype(jnp.float32)) * (1.0 / (mass + PRIOR_ONE))
    one_ref[...] = fresh.astype(jnp.bfloat16)
    moved_ref[...] = (mass * fresh).astype(jnp.bfloat16)
    mass_ref[...] = jnp.broadcast_to(mass, (tile, LANES)).T[0:1, :]


def coarse_kernel(
    n,
    moved_hbm,
    mass_ref,
    assign_ref,
    init_ref,
    two_ref,
    moved,
    sums,
    weights,
    core_out,
    core_in,
    pair_out,
    pair_in,
    line_out,
    line_in,
    held,
    mass_out,
    mass_in,
    moved_sem,
    core_sem,
    pair_sem,
    line_sem,
    mass_sem,
):
    group, me = lax.axis_index("groups"), lax.axis_index("cent")
    own, width = init_ref.shape
    local = moved.shape[0]
    lines = n // 4
    steps = lines.bit_length() - 1
    cuts = 2
    cut = own // cuts
    tile = min(512, local)
    line, pair, core = me // 4, lax.rem(me // 2, 2), lax.rem(me, 2)

    def at(z, y, c):
        return z * 4 + y * 2 + c

    load = pltpu.make_async_copy(moved_hbm, moved, moved_sem)
    load.start()
    barrier = pltpu.get_barrier_semaphore()

    @pl.loop(1, n)
    def _(off):
        peer = lax.rem(me + off, n)
        pl.semaphore_signal(barrier, inc=1, device_id=(group, peer), device_id_type=MESH)

    pl.semaphore_wait(barrier, n - 1)
    load.wait()

    def copy(src, dst, sem, slot, z, y, c):
        return pltpu.make_async_remote_copy(
            src_ref=src,
            dst_ref=dst,
            send_sem=sem.at[(0, *slot)],
            recv_sem=sem.at[(1, *slot)],
            device_id=(group, at(z, y, c)),
            device_id_type=MESH,
        )

    def core_copy(e, q):
        return copy(core_out.at[e, q], core_in.at[e, q], core_sem, (e, q), line, pair, 1 - core)

    def pair_copy(e, h):
        part = pl.ds(h * cut, cut)
        return copy(
            pair_out.at[e, part], pair_in.at[e, part], pair_sem, (e, h), line, 1 - pair, core
        )

    def line_copy(e, h):
        part = pl.ds(h * cut, cut)
        z = flip(line, e & -e, lines)
        return copy(line_out.at[e, part], line_in.at[e, part], line_sem, (e, h), z, pair, core)

    def mass_copy(peer, off):
        return pltpu.make_async_remote_copy(
            src_ref=mass_out.at[peer],
            dst_ref=mass_in.at[off],
            send_sem=mass_sem.at[0],
            recv_sem=mass_sem.at[1],
            device_id=(group, peer),
            device_id_type=MESH,
        )

    row = lax.broadcasted_iota(jnp.int32, (2 * own, 1), 0)

    def partial(e, y):
        z = flip(line, e, lines)
        theirs, ours = at(z, y, 1 - core), at(z, y, core)
        want = jnp.where(row < own, theirs * own + row, ours * own + row - own)
        sums[...] = jnp.zeros_like(sums)
        weights[...] = jnp.zeros_like(weights)

        @pl.loop(0, local // tile)
        def _(t):
            part = pl.ds(pl.multiple_of(t * tile, tile), tile)
            hit = assign_ref[:, part] == want
            value = jnp.where(hit, mass_ref[:, part], 0.0)
            fold = value[:, :LANES]
            for s in range(LANES, tile, LANES):
                fold = fold + value[:, s : s + LANES]
            weights[...] += fold
            onehot = jnp.where(hit, 1.0, 0.0).astype(jnp.bfloat16)
            sums[...] += jnp.dot(onehot, moved[part, :], preferred_element_type=jnp.float32)

        weight = jnp.sum(weights[...], axis=1, keepdims=True)
        flat = jnp.broadcast_to(weight, (2 * own, LANES)).T
        mass_out[theirs] = flat[0:1, :own]
        mass_out[ours] = flat[0:1, own:]

    def first(e):
        partial(e, 1 - pair)
        core_out[e, 0] = sums[:own, :].astype(jnp.bfloat16)
        core_copy(e, 0).start()
        held[e] = sums[own:, :]

    def swap(e):
        core_copy(e, 0).wait_recv()
        for h in range(cuts):
            part = pl.ds(h * cut, cut)
            both = held[e, part, :] + core_in[e, 0, part, :].astype(jnp.float32)
            pair_out[e, part, :] = both.astype(jnp.bfloat16)
            pair_copy(e, h).start()

    def second(e):
        partial(e, pair)
        core_out[e, 1] = sums[:own, :].astype(jnp.bfloat16)
        core_copy(e, 1).start()
        held[e] = sums[own:, :]

    def climb(e):
        core_copy(e, 1).wait_recv()
        for h in range(cuts):
            part = pl.ds(h * cut, cut)
            total = held[e, part, :] + core_in[e, 1, part, :].astype(jnp.float32)
            pair_copy(e, h).wait_recv()
            total = total + pair_in[e, part, :].astype(jnp.float32)
            for i in range(steps):
                if e % (2 << i) == 0:
                    line_copy(e + (1 << i), h).wait_recv()
                    total = total + line_in[e + (1 << i), part, :].astype(jnp.float32)
            if e > 0:
                line_out[e, part, :] = total.astype(jnp.bfloat16)
                line_copy(e, h).start()
            else:
                held[e, part, :] = total

    order = list(range(lines - 1, -1, -1))
    first(order[0])
    for s, e in enumerate(order):
        if s + 1 < lines:
            first(order[s + 1])
        swap(e)
        second(e)
        if s == lines - 1:

            @pl.loop(1, n)
            def _(off):
                mass_copy(lax.rem(me + off, n), off).start()

        if s > 0:
            climb(order[s - 1])
    climb(0)

    rest = mass_in.at[pl.ds(1, n - 1)]
    pltpu.make_async_copy(rest, rest, mass_sem.at[1]).wait()
    mass_in[0] = mass_out[me]
    weight = jnp.sum(mass_in[...], axis=0)
    eye = lax.broadcasted_iota(jnp.int32, (own, own), 0) == lax.broadcasted_iota(
        jnp.int32, (own, own), 1
    )
    weight = jnp.sum(jnp.where(eye, weight, 0.0), axis=1, keepdims=True)
    two_ref[...] = (held[0] + PRIOR_TWO * init_ref[...]) / (weight + PRIOR_TWO)

    for e in range(lines):
        core_copy(e, 0).wait_send()
        core_copy(e, 1).wait_send()
        for h in range(cuts):
            pair_copy(e, h).wait_send()
            if e > 0:
                line_copy(e, h).wait_send()
    pltpu.make_async_copy(rest, rest, mass_sem.at[0]).wait()


def shards(n, points, centroids, coarse_init, assign):
    rows, width = points.shape
    local = centroids.shape[0]
    own = coarse_init.shape[0]
    count = n * rows
    tile = min(512, local)
    lines = n // 4
    vmem = pl.BlockSpec(memory_space=pltpu.VMEM)
    anywhere = pl.BlockSpec(memory_space=pl.ANY)
    everyone, lse = pl.pallas_call(
        functools.partial(stats_kernel, n, tile),
        out_shape=(
            jax.ShapeDtypeStruct((count, width), jnp.bfloat16),
            jax.ShapeDtypeStruct((1, count), jnp.float32),
        ),
        in_specs=[vmem, anywhere],
        out_specs=(vmem, vmem),
        scratch_shapes=[
            pltpu.VMEM((local, width), jnp.bfloat16),
            pltpu.VMEM((2, 2, count // 2), jnp.float32),
            pltpu.VMEM((2, n - 1, 2, count // 2), jnp.float32),
            pltpu.SemaphoreType.DMA((local // tile,)),
            pltpu.SemaphoreType.DMA((2, lines)),
            pltpu.SemaphoreType.DMA((2, lines)),
            pltpu.SemaphoreType.DMA((2,)),
            pltpu.SemaphoreType.DMA((4,)),
        ],
        compiler_params=pltpu.CompilerParams(collective_id=0, has_side_effects=True),
        name="stats",
    )(points, centroids)
    level_one, moved, mass = pl.pallas_call(
        update_kernel,
        grid=(local // tile,),
        out_shape=(
            jax.ShapeDtypeStruct((local, width), jnp.bfloat16),
            jax.ShapeDtypeStruct((local, width), jnp.bfloat16),
            jax.ShapeDtypeStruct((1, local), jnp.float32),
        ),
        in_specs=[
            pl.BlockSpec((tile, width), lambda t: (t, 0)),
            pl.BlockSpec((count, width), lambda t: (0, 0)),
            pl.BlockSpec((1, count), lambda t: (0, 0)),
        ],
        out_specs=(
            pl.BlockSpec((tile, width), lambda t: (t, 0)),
            pl.BlockSpec((tile, width), lambda t: (t, 0)),
            pl.BlockSpec((1, tile), lambda t: (0, t)),
        ),
        name="update",
    )(centroids, everyone, lse)
    level_two = pl.pallas_call(
        functools.partial(coarse_kernel, n),
        out_shape=jax.ShapeDtypeStruct((own, width), jnp.float32),
        in_specs=[anywhere, vmem, vmem, vmem],
        out_specs=vmem,
        scratch_shapes=[
            pltpu.VMEM((local, width), jnp.bfloat16),
            pltpu.VMEM((2 * own, width), jnp.float32),
            pltpu.VMEM((2 * own, LANES), jnp.float32),
            pltpu.VMEM((lines, 2, own, width), jnp.bfloat16),
            pltpu.VMEM((lines, 2, own, width), jnp.bfloat16),
            pltpu.VMEM((lines, own, width), jnp.bfloat16),
            pltpu.VMEM((lines, own, width), jnp.bfloat16),
            pltpu.VMEM((lines, own, width), jnp.bfloat16),
            pltpu.VMEM((lines, own, width), jnp.bfloat16),
            pltpu.VMEM((lines, own, width), jnp.float32),
            pltpu.VMEM((n, 1, own), jnp.float32),
            pltpu.VMEM((n, 1, own), jnp.float32),
            pltpu.SemaphoreType.DMA,
            pltpu.SemaphoreType.DMA((2, lines, 2)),
            pltpu.SemaphoreType.DMA((2, lines, 2)),
            pltpu.SemaphoreType.DMA((2, lines, 2)),
            pltpu.SemaphoreType.DMA((2,)),
        ],
        compiler_params=pltpu.CompilerParams(collective_id=1, has_side_effects=True),
        name="coarse",
    )(moved, mass, assign.reshape(1, local), coarse_init)
    return (level_one, level_two)


def solution(mesh):
    return jax.shard_map(
        functools.partial(shards, mesh.shape["cent"]),
        mesh=mesh,
        in_specs=(
            P(("groups", "cent"), None),
            P(("groups", "cent"), None),
            P(("groups", "cent"), None),
            P(("groups", "cent")),
        ),
        out_specs=(P(("groups", "cent"), None), P(("groups", "cent"), None)),
        check_vma=False,
    )
```

time: 109 us -> 89.4 us (0.82)
  the two profiles are of different devices: /device:TPU:10 before, /device:TPU:0 now
where the time goes in v1:
time: 89.4 us; the launch traced here: 88.9 us
  Pallas kernels  86.5 us (97%)
  local copies, waits for them, and re-layouts  1.77 us (2%)
    pallas_call x1, Pallas kernels, shards(): pl.pallas_call(functools.partial(coarse_kernel, n), out_shape=jax.ShapeDt...  43.2 us
    pallas_call x1, Pallas kernels, shards(): pl.pallas_call(functools.partial(stats_kernel, n, tile), out_shape=(jax.S...  29.5 us
    pallas_call x1, Pallas kernels, shards(): pl.pallas_call(update_kernel, grid=(local // tile,), out_shape=(jax.Shape...  13.8 us

profile of v1, /device:TPU:0, one launch (start us, length us, event | category | flops | bytes accessed | tf_op | source)
XLA Modules:
  0.0 88.9 jit_solution(12343041935212526622)
XLA Ops:
  0.6 29.5 %stats.1 = (bf16[512,768]{1,0:T(8,128)(2,1)}, f32[1,512]{1,0:T(1,128)}) custom-call(bf16[32,768]{1,0:T(8,128)(2,1)} %pts_ref.1, bf16[4096,768]{1,0:T(8,128)(2,1)} %cen_ref.1), custom_call_target="tpu_custom_call" | custom-call | tf_op jit(solution)/shard_map/stats/pallas_call | solution.py:383
  30.2 13.8 %update.1 = (bf16[4096,768]{1,0:T(8,128)(2,1)}, bf16[4096,768]{1,0:T(8,128)(2,1)}, f32[1,4096]{1,0:T(1,128)}) custom-call(bf16[4096,768]{1,0:T(8,128)(2,1)} %cen_ref.1, bf16[512,768]{1,0:T(8,128)(2,1)} %get-tuple-element.7.pts_ref, f32[1,512]{1,0:T(1,128)} %get-tuple-element.8.lse_ref), custom_call_target="tpu_custom_call" | custom-call | tf_op jit(solution)/shard_map/update/pallas_call | solution.py:404
  43.9 43.2 %coarse.1 = f32[128,768]{1,0:T(8,128)} custom-call(bf16[4096,768]{1,0:T(8,128)(2,1)} %get-tuple-element.10.moved_hbm, f32[1,4096]{1,0:T(1,128)} %get-tuple-element.11.mass_ref, s32[1,4096]{1,0:T(1,128)} %bitcast.1, f32[128,768]{1,0:T(8,128)} %init_ref.1), custom_call_target="tpu_custom_call" | custom-call | tf_op jit(solution)/shard_map/coarse/pallas_call | solution.py:424
  87.1 1.8 %copy.7 = f32[128,768]{1,0:T(8,128)} copy(f32[128,768]{1,0:T(8,128)} %coarse.1) | data formatting | bytes 786432

commit v2 on v1

v2 whole, which is shorter than its diff:
```python
import functools
import math

import jax
import jax.numpy as jnp
from jax import lax
from jax.experimental import pallas as pl
from jax.experimental.pallas import tpu as pltpu
from jax.sharding import PartitionSpec as P

TEMP = 0.05
PRIOR_ONE = 0.02
PRIOR_TWO = 0.25
LANES = 128
VMEM_LIMIT = 24 << 20
MESH = pl.DeviceIdType.MESH
ROWS_BY_ROWS = (((1,), (1,)), ((), ()))


def log2_scale(width):
    return math.log2(math.e) / (TEMP * math.sqrt(width))


def flip(z, e, lines):
    out, bit = 0, 1
    while bit < lines:
        out = out + bit * lax.rem(z // bit + e // bit, 2)
        bit *= 2
    return out


def stats_kernel(
    n,
    tile,
    pts_ref,
    cen,
    all_ref,
    lse_ref,
    logits_ref,
    mine,
    theirs,
    line_sem,
    pair_sem,
    core_sem,
    sems,
):
    group, me = lax.axis_index("groups"), lax.axis_index("cent")
    rows, width = pts_ref.shape
    count = n * rows // 2
    lines = n // 4
    line, pair, core = me // 4, lax.rem(me // 2, 2), lax.rem(me, 2)
    side = line // (lines // 2)
    tiles = cen.shape[0] // tile
    c2 = log2_scale(width)

    barrier = pltpu.get_barrier_semaphore()

    @pl.loop(1, n)
    def _(off):
        peer = lax.rem(me + off, n)
        pl.semaphore_signal(barrier, inc=1, device_id=(group, peer), device_id_type=MESH)

    pl.semaphore_wait(barrier, n - 1)

    def slot(z, y, c):
        return pl.ds(pl.multiple_of((z * 4 + y * 2 + c) * rows, rows), rows)

    def send(src, where, sem, z, y, c):
        return pltpu.make_async_remote_copy(
            src_ref=src,
            dst_ref=all_ref.at[where],
            send_sem=sems.at[0],
            recv_sem=sem,
            device_id=(group, z * 4 + y * 2 + c),
            device_id_type=MESH,
        )

    def along(e, src, where):
        return send(src, where, line_sem.at[e], flip(line, e, lines), pair, core)

    def across(e, src, where):
        return send(src, where, pair_sem.at[e], line, 1 - pair, core)

    def over(e, src, where):
        return send(src, where, core_sem.at[e // (lines // 2)], line, pair, 1 - core)

    def relay_line(e):
        where = slot(flip(line, e, lines), pair, core)
        got = all_ref.at[where]
        along(e, got, where).wait_recv()
        across(e, got, where).start()
        over(e, got, where).start()

    def relay_pair(e):
        where = slot(flip(line, e, lines), 1 - pair, core)
        got = all_ref.at[where]
        across(e, got, where).wait_recv()
        over(e, got, where).start()

    def gathered(h):
        half = all_ref.at[pl.ds(0, count // 2)]
        pltpu.make_async_copy(half, half, core_sem.at[h]).wait()

    where = slot(line, pair, core)
    for e in range(lines - 1, 0, -1):
        along(e, pts_ref, where).start()
    across(0, pts_ref, where).start()
    over(0, pts_ref, where).start()
    all_ref[where, :] = pts_ref[...]

    def at(t, h):
        columns = (side + h - 2 * h * side) * count
        return (
            pl.ds(pl.multiple_of(t * tile, tile), tile),
            pl.ds(pl.multiple_of(columns, count), count),
        )

    def product(t, h, peak):
        rows_of, columns = at(t, h)
        logits = (
            lax.dot_general(
                cen[rows_of, :],
                all_ref[columns, :],
                ROWS_BY_ROWS,
                preferred_element_type=jnp.float32,
            )
            * c2
        )
        logits_ref[rows_of, columns] = logits
        return jnp.maximum(peak, jnp.max(logits.reshape(tile // 8, 8, count), axis=0))

    def exponentials(t, h, peak, total):
        power = jnp.exp2(logits_ref[at(t, h)] - peak)
        return total + jnp.sum(power.reshape(tile // 8, 8, count), axis=0)

    lowest = jnp.full((8, count), -jnp.inf, jnp.float32)
    none = jnp.zeros((8, count), jnp.float32)

    def near(t, peak):
        return product(t, 0, peak)

    def top_of(peak):
        return jnp.max(peak, axis=0, keepdims=True)

    for e in range(1, lines):
        relay_line(e)
    for e in range(lines // 2):
        relay_pair(e)
    gathered(0)
    peak = lowest
    for e in range(lines // 2):
        stop = tiles * (e + 1) // (lines // 2)
        peak = lax.fori_loop(tiles * e // (lines // 2), stop, near, peak)
        relay_pair(lines // 2 + e)
    peak0 = top_of(peak)
    total0 = lax.fori_loop(0, tiles, lambda t, total: exponentials(t, 0, peak0, total), none)
    gathered(1)
    peak1 = top_of(lax.fori_loop(0, tiles, lambda t, peak: product(t, 1, peak), lowest))
    total1 = lax.fori_loop(0, tiles, lambda t, total: exponentials(t, 1, peak1, total), none)
    for h, top, total in ((0, peak0, total0), (1, peak1, total1)):
        columns = at(0, h)[1]
        mine[0:1, columns] = top
        mine[1:2, columns] = jnp.sum(total, axis=0, keepdims=True)

    @pl.loop(1, n)
    def _(off):
        pltpu.make_async_remote_copy(
            src_ref=mine,
            dst_ref=theirs.at[off - 1],
            send_sem=sems.at[1],
            recv_sem=sems.at[2],
            device_id=(group, lax.rem(me + off, n)),
            device_id_type=MESH,
        ).start()

    pltpu.make_async_copy(theirs, theirs, sems.at[2]).wait()
    peak, total = mine[0:1, :], mine[1:2, :]
    both = theirs[...]
    top = jnp.maximum(peak, jnp.max(both[:, 0:1, :], axis=0))
    denom = total * jnp.exp2(peak - top) + jnp.sum(
        both[:, 1:2, :] * jnp.exp2(both[:, 0:1, :] - top[None]), axis=0
    )
    lse_ref[...] = top + jnp.log2(denom)
    others = all_ref.at[pl.ds(0, (n - 1) * rows)]
    pltpu.make_async_copy(others, others, sems.at[0]).wait()
    pltpu.make_async_copy(theirs, theirs, sems.at[1]).wait()


def update_kernel(
    tile, cen_ref, logits_ref, pts_ref, lse_ref, one_hbm, moved_ref, mass_ref, stage, sem
):
    local = cen_ref.shape[0]

    @pl.loop(0, local // tile)
    def _(t):
        rows = pl.ds(pl.multiple_of(t * tile, tile), tile)
        resp = jnp.exp2(logits_ref[rows, :] - lse_ref[...])
        mass = jnp.sum(resp, axis=1, keepdims=True)
        weighted = jnp.dot(
            resp.astype(jnp.bfloat16), pts_ref[...], preferred_element_type=jnp.float32
        )
        fresh = (weighted + PRIOR_ONE * cen_ref[rows, :].astype(jnp.float32)) * (
            1.0 / (mass + PRIOR_ONE)
        )
        stage[rows, :] = fresh.astype(jnp.bfloat16)
        pltpu.make_async_copy(stage.at[rows], one_hbm.at[rows], sem).start()
        moved_ref[rows, :] = (mass * fresh).astype(jnp.bfloat16)
        mass_ref[:, rows] = jnp.broadcast_to(mass, (tile, LANES)).T[0:1, :]

    pltpu.make_async_copy(stage, one_hbm, sem).wait()


def coarse_kernel(
    n,
    moved,
    mass_ref,
    assign_ref,
    init_ref,
    two_ref,
    sums,
    weights,
    core_out,
    core_in,
    pair_out,
    pair_in,
    line_out,
    line_in,
    held,
    mass_out,
    mass_in,
    core_sem,
    pair_sem,
    line_sem,
    mass_sem,
):
    group, me = lax.axis_index("groups"), lax.axis_index("cent")
    own, width = init_ref.shape
    local = moved.shape[0]
    lines = n // 4
    steps = lines.bit_length() - 1
    cuts = 2
    cut = own // cuts
    tile = min(2048, local)
    line, pair, core = me // 4, lax.rem(me // 2, 2), lax.rem(me, 2)

    def at(z, y, c):
        return z * 4 + y * 2 + c

    barrier = pltpu.get_barrier_semaphore()

    @pl.loop(1, n)
    def _(off):
        peer = lax.rem(me + off, n)
        pl.semaphore_signal(barrier, inc=1, device_id=(group, peer), device_id_type=MESH)

    def copy(src, dst, sem, slot, z, y, c):
        return pltpu.make_async_remote_copy(
            src_ref=src,
            dst_ref=dst,
            send_sem=sem.at[(0, *slot)],
            recv_sem=sem.at[(1, *slot)],
            device_id=(group, at(z, y, c)),
            device_id_type=MESH,
        )

    def core_copy(e, q):
        return copy(core_out.at[e, q], core_in.at[e, q], core_sem, (e, q), line, pair, 1 - core)

    def pair_copy(e, h):
        part = pl.ds(h * cut, cut)
        return copy(
            pair_out.at[e, part], pair_in.at[e, part], pair_sem, (e, h), line, 1 - pair, core
        )

    def line_copy(e, h):
        part = pl.ds(h * cut, cut)
        z = flip(line, e & -e, lines)
        return copy(line_out.at[e, part], line_in.at[e, part], line_sem, (e, h), z, pair, core)

    def mass_copy(peer):
        return pltpu.make_async_remote_copy(
            src_ref=mass_out.at[peer],
            dst_ref=mass_in.at[me],
            send_sem=mass_sem.at[0],
            recv_sem=mass_sem.at[1],
            device_id=(group, peer),
            device_id_type=MESH,
        )

    def partial(*owners):
        size = own * len(owners)
        row = lax.broadcasted_iota(jnp.int32, (size, 1), 0)
        want = row + owners[0] * own
        if len(owners) == 2:
            want = jnp.where(row < own, want, row - own + owners[1] * own)
        here = pl.ds(0, size)
        sums[here, :] = jnp.zeros((size, width), jnp.float32)
        weights[here, :] = jnp.zeros((size, LANES), jnp.float32)

        @pl.loop(0, local // tile)
        def _(t):
            part = pl.ds(pl.multiple_of(t * tile, tile), tile)
            hit = assign_ref[:, part] == want
            value = jnp.where(hit, mass_ref[:, part], 0.0)
            fold = value[:, :LANES]
            for s in range(LANES, tile, LANES):
                fold = fold + value[:, s : s + LANES]
            weights[here, :] += fold
            onehot = jnp.where(hit, 1.0, 0.0).astype(jnp.bfloat16)
            sums[here, :] += jnp.dot(onehot, moved[part, :], preferred_element_type=jnp.float32)

        weight = jnp.sum(weights[here, :], axis=1, keepdims=True)
        flat = jnp.broadcast_to(weight, (size, LANES)).T
        for s, owner in enumerate(owners):
            mass_out[owner] = flat[0:1, s * own : (s + 1) * own]

    def both(e, y):
        z = flip(line, e, lines)
        return at(z, y, 1 - core), at(z, y, core)

    def export(e, q):
        core_out[e, q] = sums[:own, :].astype(jnp.bfloat16)
        core_copy(e, q).start()

    def opening(e):
        theirs, ours = both(e, 1 - pair)
        partial(theirs)
        pl.semaphore_wait(barrier, n - 1)
        export(e, 0)
        mass_copy(theirs).start()
        partial(ours)
        mass_copy(ours).start()
        held[e, 0] = sums[:own, :]

    def compute(e, q):
        theirs, ours = both(e, pair if q else 1 - pair)
        partial(theirs, ours)
        export(e, q)
        mass_copy(theirs).start()
        if e > 0 or q == 0:
            mass_copy(ours).start()
        held[e, q] = sums[own:, :]

    def swap(e):
        core_copy(e, 0).wait_recv()
        for h in range(cuts):
            part = pl.ds(h * cut, cut)
            total = held[e, 0, part, :] + core_in[e, 0, part, :].astype(jnp.float32)
            pair_out[e, part, :] = total.astype(jnp.bfloat16)
            pair_copy(e, h).start()

    def climb(e, h):
        if h == 0:
            core_copy(e, 1).wait_recv()
        part = pl.ds(h * cut, cut)
        total = held[e, 1, part, :] + core_in[e, 1, part, :].astype(jnp.float32)
        pair_copy(e, h).wait_recv()
        total = total + pair_in[e, part, :].astype(jnp.float32)
        for i in range(steps):
            if e % (2 << i) == 0:
                line_copy(e + (1 << i), h).wait_recv()
                total = total + line_in[e + (1 << i), part, :].astype(jnp.float32)
        if e > 0:
            line_out[e, part, :] = total.astype(jnp.bfloat16)
            line_copy(e, h).start()
        else:
            held[e, 1, part, :] = total

    order = list(range(lines - 1, -1, -1))
    opening(order[0])
    swap(order[0])
    for s, e in enumerate(order):
        if s + 1 < lines:
            compute(order[s + 1], 0)
        if s > 0:
            climb(order[s - 1], 1)
        compute(e, 1)
        if s + 1 < lines:
            swap(order[s + 1])
        climb(e, 0)
    climb(0, 1)

    rest = mass_in.at[pl.ds(1, n - 1)]
    pltpu.make_async_copy(rest, rest, mass_sem.at[1]).wait()
    mass_in[me] = mass_out[me]
    weight = jnp.sum(mass_in[...], axis=0)
    eye = lax.broadcasted_iota(jnp.int32, (own, own), 0) == lax.broadcasted_iota(
        jnp.int32, (own, own), 1
    )
    weight = jnp.sum(jnp.where(eye, weight, 0.0), axis=1, keepdims=True)
    two_ref[...] = (held[0, 1] + PRIOR_TWO * init_ref[...]) / (weight + PRIOR_TWO)

    for e in range(lines):
        core_copy(e, 0).wait_send()
        core_copy(e, 1).wait_send()
        for h in range(cuts):
            pair_copy(e, h).wait_send()
            if e > 0:
                line_copy(e, h).wait_send()
    pltpu.make_async_copy(rest, rest, mass_sem.at[0]).wait()


def shards(n, points, centroids, coarse_init, assign):
    rows, width = points.shape
    local = centroids.shape[0]
    own = coarse_init.shape[0]
    count = n * rows
    tile = min(1024, local)
    lines = n // 4
    vmem = pl.BlockSpec(memory_space=pltpu.VMEM)
    anywhere = pl.BlockSpec(memory_space=pl.ANY)
    everyone, lse, logits = pl.pallas_call(
        functools.partial(stats_kernel, n, tile),
        out_shape=(
            jax.ShapeDtypeStruct((count, width), jnp.bfloat16),
            jax.ShapeDtypeStruct((1, count), jnp.float32),
            jax.ShapeDtypeStruct((local, count), jnp.float32),
        ),
        in_specs=[vmem, vmem],
        out_specs=(vmem, vmem, vmem),
        scratch_shapes=[
            pltpu.VMEM((2, count), jnp.float32),
            pltpu.VMEM((n - 1, 2, count), jnp.float32),
            pltpu.SemaphoreType.DMA((lines,)),
            pltpu.SemaphoreType.DMA((lines,)),
            pltpu.SemaphoreType.DMA((2,)),
            pltpu.SemaphoreType.DMA((3,)),
        ],
        compiler_params=pltpu.CompilerParams(
            collective_id=0, has_side_effects=True, vmem_limit_bytes=VMEM_LIMIT
        ),
        name="stats",
    )(points, centroids)
    chunk = min(local, max(64, tile * 256 // count))
    level_one, moved, mass = pl.pallas_call(
        functools.partial(update_kernel, chunk),
        out_shape=(
            jax.ShapeDtypeStruct((local, width), jnp.bfloat16),
            jax.ShapeDtypeStruct((local, width), jnp.bfloat16),
            jax.ShapeDtypeStruct((1, local), jnp.float32),
        ),
        in_specs=[vmem, vmem, vmem, vmem],
        out_specs=(anywhere, vmem, vmem),
        scratch_shapes=[
            pltpu.VMEM((local, width), jnp.bfloat16),
            pltpu.SemaphoreType.DMA,
        ],
        compiler_params=pltpu.CompilerParams(vmem_limit_bytes=VMEM_LIMIT),
        name="update",
    )(centroids, logits, everyone, lse)
    level_two = pl.pallas_call(
        functools.partial(coarse_kernel, n),
        out_shape=jax.ShapeDtypeStruct((own, width), jnp.float32),
        in_specs=[vmem, vmem, vmem, vmem],
        out_specs=vmem,
        scratch_shapes=[
            pltpu.VMEM((2 * own, width), jnp.float32),
            pltpu.VMEM((2 * own, LANES), jnp.float32),
            pltpu.VMEM((lines, 2, own, width), jnp.bfloat16),
            pltpu.VMEM((lines, 2, own, width), jnp.bfloat16),
            pltpu.VMEM((lines, own, width), jnp.bfloat16),
            pltpu.VMEM((lines, own, width), jnp.bfloat16),
            pltpu.VMEM((lines, own, width), jnp.bfloat16),
            pltpu.VMEM((lines, own, width), jnp.bfloat16),
            pltpu.VMEM((lines, 2, own, width), jnp.float32),
            pltpu.VMEM((n, 1, own), jnp.float32),
            pltpu.VMEM((n, 1, own), jnp.float32),
            pltpu.SemaphoreType.DMA((2, lines, 2)),
            pltpu.SemaphoreType.DMA((2, lines, 2)),
            pltpu.SemaphoreType.DMA((2, lines, 2)),
            pltpu.SemaphoreType.DMA((2,)),
        ],
        compiler_params=pltpu.CompilerParams(
            collective_id=1, has_side_effects=True, vmem_limit_bytes=VMEM_LIMIT
        ),
        name="coarse",
    )(moved, mass, assign.reshape(1, local), coarse_init)
    return (level_one, level_two)


def solution(mesh):
    return jax.shard_map(
        functools.partial(shards, mesh.shape["cent"]),
        mesh=mesh,
        in_specs=(
            P(("groups", "cent"), None),
            P(("groups", "cent"), None),
            P(("groups", "cent"), None),
            P(("groups", "cent")),
        ),
        out_specs=(P(("groups", "cent"), None), P(("groups", "cent"), None)),
        check_vma=False,
    )
```

time: 89.4 us -> 68 us (0.76)
  Pallas kernels: 86.5 us -> 62.8 us
  local copies, waits for them, and re-layouts: 1.77 us -> 4.34 us
    pallas_call x1, Pallas kernels: 43.2 us -> 31.2 us  [shards(): pl.pallas_call(functools.partial(coarse_kernel, n), out_shape=jax.ShapeDt...]
    pallas_call x1, Pallas kernels: 13.8 us -> 6.18 us  [shards(): pl.pallas_call(functools.partial(update_kernel, chunk), out_shape=(jax.Sh...]
    pallas_call x1, Pallas kernels: 29.5 us -> 25.4 us  [shards(): pl.pallas_call(functools.partial(stats_kernel, n, tile), out_shape=(jax.S...]
    unnamed x1 -> x11, local copies, waits for them, and re-layouts: 1.77 us -> 4.34 us
where the time goes in v2:
time: 68 us; the launch traced here: 67.8 us
  Pallas kernels  62.8 us (92%)
  local copies, waits for them, and re-layouts  4.34 us (6%)
  between operations  0.7 us (1%)
    pallas_call x1, Pallas kernels, shards(): pl.pallas_call(functools.partial(coarse_kernel, n), out_shape=jax.ShapeDt...  31.2 us
    pallas_call x1, Pallas kernels, shards(): pl.pallas_call(functools.partial(stats_kernel, n, tile), out_shape=(jax.S...  25.4 us
    pallas_call x1, Pallas kernels, shards(): pl.pallas_call(functools.partial(update_kernel, chunk), out_shape=(jax.Sh...  6.18 us
    unnamed x11, local copies, waits for them, and re-layouts  4.34 us

profile of v2, /device:TPU:0, one launch (start us, length us, event | category | flops | bytes accessed | tf_op | source)
XLA Modules:
  0.0 67.8 jit_solution(9824877048399939942)
XLA Ops:
  0.6 0.0 copy-start
  0.6 2.8 %copy-done = bf16[4096,768]{1,0:T(8,128)(2,1)S(1)} copy-done((bf16[4096,768]{1,0:T(8,128)(2,1)S(1)}, bf16[4096,768]{1,0:T(8,128)(2,1)}, u32[]{:S(2)}) %copy-start) | copy-done | bytes 6291480
  3.4 0.0 copy-start.3
  3.4 0.8 %copy-done.3 = bf16[32,768]{1,0:T(8,128)(2,1)S(1)} copy-done((bf16[32,768]{1,0:T(8,128)(2,1)S(1)}, bf16[32,768]{1,0:T(8,128)(2,1)}, u32[]{:S(2)}) %copy-start.3) | copy-done | bytes 49176
  4.2 0.0 copy-start.1
  4.2 25.4 %stats.1 = (bf16[512,768]{1,0:T(8,128)(2,1)S(1)}, f32[1,512]{1,0:T(1,128)S(1)}, f32[4096,512]{1,0:T(8,128)S(1)}) custom-call(bf16[32,768]{1,0:T(8,128)(2,1)S(1)} %copy-done.3, bf16[4096,768]{1,0:T(8,128)(2,1)S(1)} %copy-done), custom_call_target="tpu_custom_call" | custom-call | tf_op jit(solution)/shard_map/stats/pallas_call | solution.py:412
  29.6 0.0 copy-done.1
  29.6 0.0 copy-start.2
  29.6 0.0 copy-start.4
  29.6 6.2 %update.1 = (bf16[4096,768]{1,0:T(8,128)(2,1)}, bf16[4096,768]{1,0:T(8,128)(2,1)S(1)}, f32[1,4096]{1,0:T(1,128)S(1)}) custom-call(bf16[4096,768]{1,0:T(8,128)(2,1)S(1)} %copy-done.1, f32[4096,512]{1,0:T(8,128)S(1)} %get-tuple-element.8.logits_ref, bf16[512,768]{1,0:T(8,128)(2,1)S(1)} %get-tuple-element.9.pts_ref, f32[1,512]{1,0:T(1,128)S(1)} %get-tuple-element.10.lse_ref), custom_call_target="tpu_custom_call" | custom-call | tf_op jit(solution)/shard_map/update/pallas_call | solution.py:435
  35.8 0.0 copy-done.2
  35.8 0.0 copy-done.4
  35.8 31.2 %coarse.1 = f32[128,768]{1,0:T(8,128)S(1)} custom-call(bf16[4096,768]{1,0:T(8,128)(2,1)S(1)} %get-tuple-element.12.moved, f32[1,4096]{1,0:T(1,128)S(1)} %get-tuple-element.13.mass_ref, s32[1,4096]{1,0:T(1,128)S(1)} %bitcast.1, f32[128,768]{1,0:T(8,128)S(1)} %copy-done.2), custom_call_target="tpu_custom_call" | custom-call | tf_op jit(solution)/shard_map/coarse/pallas_call | solution.py:451
  67.1 0.7 %copy.7 = f32[128,768]{1,0:T(8,128)} copy(f32[128,768]{1,0:T(8,128)S(1)} %coarse.1) | data formatting | bytes 786432
Async XLA Ops:
  0.6 2.8 %copy-start = (bf16[4096,768]{1,0:T(8,128)(2,1)S(1)}, bf16[4096,768]{1,0:T(8,128)(2,1)}, u32[]{:S(2)}) copy-start(bf16[4096,768]{1,0:T(8,128)(2,1)} %cen_ref.1) | copy-start | bytes 18874372
  3.4 0.8 %copy-start.3 = (bf16[32,768]{1,0:T(8,128)(2,1)S(1)}, bf16[32,768]{1,0:T(8,128)(2,1)}, u32[]{:S(2)}) copy-start(bf16[32,768]{1,0:T(8,128)(2,1)} %pts_ref.1) | copy-start | bytes 147460
  4.2 25.4 %copy-start.1 = (bf16[4096,768]{1,0:T(8,128)(2,1)S(1)}, bf16[4096,768]{1,0:T(8,128)(2,1)}, u32[]{:S(2)}) copy-start(bf16[4096,768]{1,0:T(8,128)(2,1)} %cen_ref.1) | copy-start | bytes 18874372
  29.6 6.2 %copy-start.2 = (f32[128,768]{1,0:T(8,128)S(1)}, f32[128,768]{1,0:T(8,128)}, u32[]{:S(2)}) copy-start(f32[128,768]{1,0:T(8,128)} %init_ref.1) | copy-start | bytes 1179652
  29.6 6.2 %copy-start.4 = (s32[4096]{0:T(1024)S(1)}, s32[4096]{0:T(1024)}, u32[]{:S(2)}) copy-start(s32[4096]{0:T(1024)} %param.7) | copy-start | bytes 49156

commit v3 on v2

--- a/solution.py
+++ b/solution.py
@@ -272,9 +272,12 @@
             pair_out.at[e, part], pair_in.at[e, part], pair_sem, (e, h), line, 1 - pair, core
         )
 
-    def line_copy(e, h):
+    forward = lines == 4
+    inner = lax.rem(line // 2 + line, 2) == 1
+
+    def line_copy(e, h, away=None):
         part = pl.ds(h * cut, cut)
-        z = flip(line, e & -e, lines)
+        z = flip(line, e & -e if away is None else away, lines)
         return copy(line_out.at[e, part], line_in.at[e, part], line_sem, (e, h), z, pair, core)
 
     def mass_copy(peer):
@@ -349,13 +352,56 @@
             pair_out[e, part, :] = total.astype(jnp.bfloat16)
             pair_copy(e, h).start()
 
-    def climb(e, h):
+    def base(e, h):
         if h == 0:
             core_copy(e, 1).wait_recv()
         part = pl.ds(h * cut, cut)
         total = held[e, 1, part, :] + core_in[e, 1, part, :].astype(jnp.float32)
         pair_copy(e, h).wait_recv()
-        total = total + pair_in[e, part, :].astype(jnp.float32)
+        return total + pair_in[e, part, :].astype(jnp.float32)
+
+    def pass_on(slot, h, away, total):
+        line_out[slot, pl.ds(h * cut, cut), :] = total.astype(jnp.bfloat16)
+        line_copy(slot, h, away).start()
+
+    def arrived(slot, h):
+        line_copy(slot, h, 1).wait_recv()
+        return line_in[slot, pl.ds(h * cut, cut), :].astype(jnp.float32)
+
+    def climb_four(e, h):
+        part = pl.ds(h * cut, cut)
+        if e == 1:
+
+            @pl.when(inner)
+            def _():
+                pass_on(0, h, 3, held[3, 1, part, :] + arrived(2, h))
+
+        held[e, 1, part, :] = base(e, h)
+        if e == 0:
+            held[e, 1, part, :] += arrived(1, h)
+
+        @pl.when(inner)
+        def _():
+            if e == 2:
+                pass_on(2, h, 2, held[e, 1, part, :] + arrived(3, h))
+            elif e == 1:
+                pass_on(1, h, 1, held[e, 1, part, :])
+            elif e == 0:
+                held[e, 1, part, :] += arrived(0, h)
+
+        @pl.when(jnp.logical_not(inner))
+        def _():
+            if e > 0:
+                pass_on(e, h, 1, held[e, 1, part, :])
+            else:
+                held[e, 1, part, :] += arrived(2, h)
+
+    def climb(e, h):
+        if forward:
+            climb_four(e, h)
+            return
+        part = pl.ds(h * cut, cut)
+        total = base(e, h)
         for i in range(steps):
             if e % (2 << i) == 0:
                 line_copy(e + (1 << i), h).wait_recv()
@@ -395,7 +441,13 @@
         core_copy(e, 1).wait_send()
         for h in range(cuts):
             pair_copy(e, h).wait_send()
-            if e > 0:
+            if forward and e in (0, 3):
+
+                @pl.when(inner if e == 0 else jnp.logical_not(inner))
+                def _(e=e, h=h):
+                    line_copy(e, h, 1).wait_send()
+
+            elif e > 0:
                 line_copy(e, h).wait_send()
     pltpu.make_async_copy(rest, rest, mass_sem.at[0]).wait()
 

time: 68 us -> 65.8 us (0.968)
  Pallas kernels: 62.8 us -> 60.6 us
    pallas_call x1, Pallas kernels: 31.2 us -> 29.1 us  [shards(): pl.pallas_call(functools.partial(coarse_kernel, n), out_shape=jax.ShapeDt...]
where the time goes in v3:
time: 65.8 us; the launch traced here: 65.6 us
  Pallas kernels  60.6 us (92%)
  local copies, waits for them, and re-layouts  4.34 us (7%)
  between operations  0.7 us (1%)
    pallas_call x1, Pallas kernels, shards(): pl.pallas_call(functools.partial(coarse_kernel, n), out_shape=jax.ShapeDt...  29.1 us
    pallas_call x1, Pallas kernels, shards(): pl.pallas_call(functools.partial(stats_kernel, n, tile), out_shape=(jax.S...  25.4 us
    pallas_call x1, Pallas kernels, shards(): pl.pallas_call(functools.partial(update_kernel, chunk), out_shape=(jax.Sh...  6.18 us
    unnamed x11, local copies, waits for them, and re-layouts  4.34 us

profile of v3, /device:TPU:0, one launch (start us, length us, event | category | flops | bytes accessed | tf_op | source)
XLA Modules:
  0.0 65.6 jit_solution(13214039452804922002)
XLA Ops:
  0.6 0.0 copy-start
  0.6 2.8 %copy-done = bf16[4096,768]{1,0:T(8,128)(2,1)S(1)} copy-done((bf16[4096,768]{1,0:T(8,128)(2,1)S(1)}, bf16[4096,768]{1,0:T(8,128)(2,1)}, u32[]{:S(2)}) %copy-start) | copy-done | bytes 6291480
  3.4 0.0 copy-start.3
  3.4 0.8 %copy-done.3 = bf16[32,768]{1,0:T(8,128)(2,1)S(1)} copy-done((bf16[32,768]{1,0:T(8,128)(2,1)S(1)}, bf16[32,768]{1,0:T(8,128)(2,1)}, u32[]{:S(2)}) %copy-start.3) | copy-done | bytes 49176
  4.2 0.0 copy-start.1
  4.2 25.4 %stats.1 = (bf16[512,768]{1,0:T(8,128)(2,1)S(1)}, f32[1,512]{1,0:T(1,128)S(1)}, f32[4096,512]{1,0:T(8,128)S(1)}) custom-call(bf16[32,768]{1,0:T(8,128)(2,1)S(1)} %copy-done.3, bf16[4096,768]{1,0:T(8,128)(2,1)S(1)} %copy-done), custom_call_target="tpu_custom_call" | custom-call | tf_op jit(solution)/shard_map/stats/pallas_call | solution.py:464
  29.6 0.0 copy-done.1
  29.6 0.0 copy-start.2
  29.6 0.0 copy-start.4
  29.6 6.2 %update.1 = (bf16[4096,768]{1,0:T(8,128)(2,1)}, bf16[4096,768]{1,0:T(8,128)(2,1)S(1)}, f32[1,4096]{1,0:T(1,128)S(1)}) custom-call(bf16[4096,768]{1,0:T(8,128)(2,1)S(1)} %copy-done.1, f32[4096,512]{1,0:T(8,128)S(1)} %get-tuple-element.8.logits_ref, bf16[512,768]{1,0:T(8,128)(2,1)S(1)} %get-tuple-element.9.pts_ref, f32[1,512]{1,0:T(1,128)S(1)} %get-tuple-element.10.lse_ref), custom_call_target="tpu_custom_call" | custom-call | tf_op jit(solution)/shard_map/update/pallas_call | solution.py:487
  35.8 0.0 copy-done.2
  35.8 0.0 copy-done.4
  35.8 29.1 %coarse.1 = f32[128,768]{1,0:T(8,128)S(1)} custom-call(bf16[4096,768]{1,0:T(8,128)(2,1)S(1)} %get-tuple-element.12.moved, f32[1,4096]{1,0:T(1,128)S(1)} %get-tuple-element.13.mass_ref, s32[1,4096]{1,0:T(1,128)S(1)} %bitcast.1, f32[128,768]{1,0:T(8,128)S(1)} %copy-done.2), custom_call_target="tpu_custom_call" | custom-call | tf_op jit(solution)/shard_map/coarse/pallas_call | solution.py:503
  64.9 0.7 %copy.7 = f32[128,768]{1,0:T(8,128)} copy(f32[128,768]{1,0:T(8,128)S(1)} %coarse.1) | data formatting | bytes 786432
Async XLA Ops:
  0.6 2.8 %copy-start = (bf16[4096,768]{1,0:T(8,128)(2,1)S(1)}, bf16[4096,768]{1,0:T(8,128)(2,1)}, u32[]{:S(2)}) copy-start(bf16[4096,768]{1,0:T(8,128)(2,1)} %cen_ref.1) | copy-start | bytes 18874372
  3.4 0.8 %copy-start.3 = (bf16[32,768]{1,0:T(8,128)(2,1)S(1)}, bf16[32,768]{1,0:T(8,128)(2,1)}, u32[]{:S(2)}) copy-start(bf16[32,768]{1,0:T(8,128)(2,1)} %pts_ref.1) | copy-start | bytes 147460
  4.2 25.4 %copy-start.1 = (bf16[4096,768]{1,0:T(8,128)(2,1)S(1)}, bf16[4096,768]{1,0:T(8,128)(2,1)}, u32[]{:S(2)}) copy-start(bf16[4096,768]{1,0:T(8,128)(2,1)} %cen_ref.1) | copy-start | bytes 18874372
  29.6 6.2 %copy-start.2 = (f32[128,768]{1,0:T(8,128)S(1)}, f32[128,768]{1,0:T(8,128)}, u32[]{:S(2)}) copy-start(f32[128,768]{1,0:T(8,128)} %init_ref.1) | copy-start | bytes 1179652
  29.6 6.2 %copy-start.4 = (s32[4096]{0:T(1024)S(1)}, s32[4096]{0:T(1024)}, u32[]{:S(2)}) copy-start(s32[4096]{0:T(1024)} %param.7) | copy-start | bytes 49156

commit v4 on v3

--- a/solution.py
+++ b/solution.py
@@ -457,7 +457,7 @@
     local = centroids.shape[0]
     own = coarse_init.shape[0]
     count = n * rows
-    tile = min(1024, local)
+    tile = min(2048, local)
     lines = n // 4
     vmem = pl.BlockSpec(memory_space=pltpu.VMEM)
     anywhere = pl.BlockSpec(memory_space=pl.ANY)
@@ -483,7 +483,7 @@
         ),
         name="stats",
     )(points, centroids)
-    chunk = min(local, max(64, tile * 256 // count))
+    chunk = min(local, max(LANES, tile * 128 // count))
     level_one, moved, mass = pl.pallas_call(
         functools.partial(update_kernel, chunk),
         out_shape=(

time: 65.8 us -> 66.8 us (1.015)
  Pallas kernels: 60.6 us -> 61.5 us
    pallas_call x1, Pallas kernels: 25.4 us -> 26.1 us  [shards(): pl.pallas_call(functools.partial(stats_kernel, n, tile), out_shape=(jax.S...]
where the time goes in v4:
time: 66.8 us; the launch traced here: 66.6 us
  Pallas kernels  61.5 us (92%)
  local copies, waits for them, and re-layouts  4.34 us (6%)
  between operations  0.7 us (1%)
    pallas_call x1, Pallas kernels, shards(): pl.pallas_call(functools.partial(coarse_kernel, n), out_shape=jax.ShapeDt...  29.2 us
    pallas_call x1, Pallas kernels, shards(): pl.pallas_call(functools.partial(stats_kernel, n, tile), out_shape=(jax.S...  26.1 us
    pallas_call x1, Pallas kernels, shards(): pl.pallas_call(functools.partial(update_kernel, chunk), out_shape=(jax.Sh...  6.17 us
    unnamed x11, local copies, waits for them, and re-layouts  4.34 us

profile of v4, /device:TPU:0, one launch (start us, length us, event | category | flops | bytes accessed | tf_op | source)
XLA Modules:
  0.0 66.6 jit_solution(12950794551436963391)
XLA Ops:
  0.6 0.0 copy-start
  0.6 2.8 %copy-done = bf16[4096,768]{1,0:T(8,128)(2,1)S(1)} copy-done((bf16[4096,768]{1,0:T(8,128)(2,1)S(1)}, bf16[4096,768]{1,0:T(8,128)(2,1)}, u32[]{:S(2)}) %copy-start) | copy-done | bytes 6291480
  3.4 0.0 copy-start.3
  3.4 0.8 %copy-done.3 = bf16[32,768]{1,0:T(8,128)(2,1)S(1)} copy-done((bf16[32,768]{1,0:T(8,128)(2,1)S(1)}, bf16[32,768]{1,0:T(8,128)(2,1)}, u32[]{:S(2)}) %copy-start.3) | copy-done | bytes 49176
  4.2 0.0 copy-start.1
  4.2 26.1 %stats.1 = (bf16[512,768]{1,0:T(8,128)(2,1)S(1)}, f32[1,512]{1,0:T(1,128)S(1)}, f32[4096,512]{1,0:T(8,128)S(1)}) custom-call(bf16[32,768]{1,0:T(8,128)(2,1)S(1)} %copy-done.3, bf16[4096,768]{1,0:T(8,128)(2,1)S(1)} %copy-done), custom_call_target="tpu_custom_call" | custom-call | tf_op jit(solution)/shard_map/stats/pallas_call | solution.py:464
  30.3 0.0 copy-done.1
  30.3 0.0 copy-start.2
  30.4 0.0 copy-start.4
  30.4 6.2 %update.1 = (bf16[4096,768]{1,0:T(8,128)(2,1)}, bf16[4096,768]{1,0:T(8,128)(2,1)S(1)}, f32[1,4096]{1,0:T(1,128)S(1)}) custom-call(bf16[4096,768]{1,0:T(8,128)(2,1)S(1)} %copy-done.1, f32[4096,512]{1,0:T(8,128)S(1)} %get-tuple-element.8.logits_ref, bf16[512,768]{1,0:T(8,128)(2,1)S(1)} %get-tuple-element.9.pts_ref, f32[1,512]{1,0:T(1,128)S(1)} %get-tuple-element.10.lse_ref), custom_call_target="tpu_custom_call" | custom-call | tf_op jit(solution)/shard_map/update/pallas_call | solution.py:487
  36.5 0.0 copy-done.2
  36.6 0.0 copy-done.4
  36.6 29.2 %coarse.1 = f32[128,768]{1,0:T(8,128)S(1)} custom-call(bf16[4096,768]{1,0:T(8,128)(2,1)S(1)} %get-tuple-element.12.moved, f32[1,4096]{1,0:T(1,128)S(1)} %get-tuple-element.13.mass_ref, s32[1,4096]{1,0:T(1,128)S(1)} %bitcast.1, f32[128,768]{1,0:T(8,128)S(1)} %copy-done.2), custom_call_target="tpu_custom_call" | custom-call | tf_op jit(solution)/shard_map/coarse/pallas_call | solution.py:503
  65.8 0.7 %copy.7 = f32[128,768]{1,0:T(8,128)} copy(f32[128,768]{1,0:T(8,128)S(1)} %coarse.1) | data formatting | bytes 786432
Async XLA Ops:
  0.6 2.8 %copy-start = (bf16[4096,768]{1,0:T(8,128)(2,1)S(1)}, bf16[4096,768]{1,0:T(8,128)(2,1)}, u32[]{:S(2)}) copy-start(bf16[4096,768]{1,0:T(8,128)(2,1)} %cen_ref.1) | copy-start | bytes 18874372
  3.4 0.8 %copy-start.3 = (bf16[32,768]{1,0:T(8,128)(2,1)S(1)}, bf16[32,768]{1,0:T(8,128)(2,1)}, u32[]{:S(2)}) copy-start(bf16[32,768]{1,0:T(8,128)(2,1)} %pts_ref.1) | copy-start | bytes 147460
  4.2 26.1 %copy-start.1 = (bf16[4096,768]{1,0:T(8,128)(2,1)S(1)}, bf16[4096,768]{1,0:T(8,128)(2,1)}, u32[]{:S(2)}) copy-start(bf16[4096,768]{1,0:T(8,128)(2,1)} %cen_ref.1) | copy-start | bytes 18874372
  30.3 6.2 %copy-start.2 = (f32[128,768]{1,0:T(8,128)S(1)}, f32[128,768]{1,0:T(8,128)}, u32[]{:S(2)}) copy-start(f32[128,768]{1,0:T(8,128)} %init_ref.1) | copy-start | bytes 1179652
  30.4 6.2 %copy-start.4 = (s32[4096]{0:T(1024)S(1)}, s32[4096]{0:T(1024)}, u32[]{:S(2)}) copy-start(s32[4096]{0:T(1024)} %param.7) | copy-start | bytes 49156
